TPU v7x, 512 devices: a whole 4x8x8 slice. The times are simulated.
512 devices in a mesh: gx: 32 (over x_lo, z, core), yz: 16 (over x_hi, y).
Axes of the slice: x: 4 (x_hi: 2, x_lo: 2; x = x_hi * 2 + x_lo), y: 8, z: 8, core: 2. Of those that a mesh axis runs over, the one named last changes fastest.
Arguments:
- leaf_moments: bfloat16 [256, 128, 256], P('gx', 'yz'), may hold values from -6 to 6
- leaf_list: int32 [256, 128, 16], P('gx', 'yz'), may hold values from 0 to 288
- leaf_op: int32 [256, 128, 16], P('gx', 'yz'), may hold values from 0 to 15
- leaf_parent: int32 [256, 128], P('gx', 'yz'), may hold values from 0 to 127, as said below
- leaf_octant: int32 [256, 128], P('gx', 'yz'), may hold values from 0 to 7, as said below
- parent_list: int32 [32, 128, 8], P('gx', 'yz'), may hold values from 0 to 639
- parent_op: int32 [32, 128, 8], P('gx', 'yz'), may hold values from 0 to 15
- operators: bfloat16 [16, 256, 256], replicated, may hold values from -0.09375 to 0.09375
- shift_up: bfloat16 [8, 256, 256], replicated, may hold values from -0.125 to 0.125
- density: bfloat16 [8192, 128, 128], P(('gx', 'yz')), may hold values from -6 to 6
- nearby_coulomb_kernel: bfloat16 [8, 128, 128], replicated, may hold values from -0.1875 to 0.1875
- near_src: int32 [8192, 16], P(('gx', 'yz')), may hold values from 0 to 15
- near_kind: int32 [8192, 16], P(('gx', 'yz')), may hold values from 0 to 7
- near_count: int32 [8192], P(('gx', 'yz')), may hold values from 1 to 16
- eval_rows: float32 [128, 16], replicated, may hold values from -1.5 to 1.5
- eval_cols: float32 [16, 128], replicated, may hold values from -1.5 to 1.5
Outputs:
- coulomb: bfloat16 [8192, 128, 128], P(('gx', 'yz'))
Inputs may be any that keep to these rules, and one draw needn't show every extreme that they name: `leaf_parent`: within each column of leaf blocks (a // 8 fixed) every coarse box number is named by exactly 8 leaves. `leaf_octant`: the 8 leaves of one coarse box have 8 different octants.
All inputs are finite; a program needn't handle non-finite values.
Results may differ from a plain program's by a relative error of at most 0.0026.
Values may be sent and summed in bfloat16 or wider, within the bound.
No kernel may reach another device: no remote copies, remote signals or barrier semaphores. Data moves between devices by JAX's collectives and lax.ppermute only.
A program may use at most 64 MiB of HBM per device.

v0:
```python
import jax
import jax.numpy as jnp
from jax import lax
from jax.experimental import pallas as pl
from jax.experimental.pallas import tpu as pltpu
from jax.sharding import PartitionSpec as P

BF16 = jnp.bfloat16
F32 = jnp.float32
LEAVES = 64
ROWS = 136
COEFFS = 256
HALF = 128
BLOCKS = 3 * LEAVES
PARENTS = 128
OPS = 16
OCTANTS = 8
SLOTS = 16
PSLOTS = 8
MIB = 1024 * 1024


def dot(a, b):
    return jnp.dot(a, b, preferred_element_type=F32)


def dot_rows(a, b):
    return lax.dot_general(a, b, (((1,), (1,)), ((), ())), preferred_element_type=F32)


def one_hot(labels, positions):
    return jnp.where(labels == positions, 1.0, 0.0).astype(BF16)


def halves(x):
    high = x.astype(BF16)
    return high, (x - high.astype(F32)).astype(BF16)


def near_field(src_ref, kind_ref, count_ref, density_ref, kinds_ref, out_ref, products):
    kinds_count, side, _ = kinds_ref.shape
    tiles = density_ref.shape[0]
    stacked = kinds_ref[...].reshape(kinds_count * side, side)

    @pl.loop(0, tiles // 2)
    def _(pair):
        both = jnp.concatenate([density_ref[2 * pair], density_ref[2 * pair + 1]], axis=1)
        made = dot(stacked, both)
        for half in range(2):
            products[2 * pair + half] = made[:, half * side : (half + 1) * side].reshape(
                kinds_count, side, side
            )

    @pl.loop(0, tiles)
    def _(tile):
        def add(slot, total):
            return total + products[src_ref[tile, slot], kind_ref[tile, slot]]

        out_ref[tile] = lax.fori_loop(
            0, count_ref[tile], add, jnp.zeros((side, side), F32)
        )


def payload_kernel(*refs):
    sources, out_ref, held, block, in_sem, out_sem = refs[:5], refs[5], refs[6:11], *refs[11:]
    fetches = [
        pltpu.make_async_copy(source, target, in_sem.at[number])
        for number, (source, target) in enumerate(zip(sources, held))
    ]
    for fetch in fetches:
        fetch.start()
    fetches[0].wait()
    moments_ref, parent_ref, octant_ref, list_ref, op_ref = held
    block[:LEAVES, :] = moments_ref[:, :HALF]
    block[LEAVES : 2 * LEAVES, :] = moments_ref[:, HALF:]
    peers = out_ref.shape[0]
    stores = []
    for part, rows in enumerate((slice(0, 2 * LEAVES), slice(2 * LEAVES, ROWS))):
        stores.append(
            [
                pltpu.make_async_copy(
                    block.at[rows], out_ref.at[peer, rows], out_sem.at[part, peer]
                )
                for peer in range(peers)
            ]
        )
    for store in stores[0]:
        store.start()
    for fetch in fetches[1:]:
        fetch.wait()
    coarse = list_ref[...]
    numbers = jnp.concatenate(
        [parent_ref[...], octant_ref[...], coarse >> 7, coarse & 127, op_ref[...]], axis=0
    )
    count, side = numbers.shape
    lane = lax.broadcasted_iota(jnp.int32, (side, LEAVES), 1)
    spread = dot(
        numbers.astype(F32).astype(BF16),
        one_hot(lane % side, lax.broadcasted_iota(jnp.int32, (side, LEAVES), 0)),
    )
    lane = lax.broadcasted_iota(jnp.int32, (count, LEAVES), 1)
    row = lax.broadcasted_iota(jnp.int32, (count, LEAVES), 0)
    kept = jnp.where(lane // side == row % side, spread, 0.0)
    rows = [
        jnp.sum(kept[number * side : (number + 1) * side], axis=0, keepdims=True)
        for number in range(count // side)
    ]
    blank = jnp.zeros((1, LEAVES), F32)
    lines = [
        jnp.concatenate(pair, axis=1)
        for pair in ((rows[0], blank), (rows[1], blank), (rows[2], rows[3]), (rows[4], blank))
    ]
    lines = jnp.concatenate(lines + [jnp.zeros((4, 2 * LEAVES), F32)], axis=0).astype(BF16)
    block[2 * LEAVES :, :] = lines
    for store in stores[1]:
        store.start()
    for store in stores[0] + stores[1]:
        store.wait()


def count_tables(parity_ref, list_ref, op_ref, counts_ref):
    leaf_list = list_ref[...]
    side = 8
    span = 2 * side + 1
    leaf = lax.broadcasted_iota(jnp.int32, leaf_list.shape, 0)
    first = leaf // side + leaf_list // span
    second = leaf % side + leaf_list % span
    codes = (
        (first // side) * BLOCKS
        + (second // side) * LEAVES
        + (first % side) * side
        + second % side
    )
    square = (SLOTS, SLOTS)
    eye = one_hot(
        lax.broadcasted_iota(jnp.int32, square, 0), lax.broadcasted_iota(jnp.int32, square, 1)
    )
    rows = op_rows(dot_rows(eye, op_ref[...].astype(F32).astype(BF16)), 0, SLOTS)
    chosen = operator_masks(rows, SLOTS)
    place = lax.broadcasted_iota(jnp.int32, (LEAVES, BLOCKS), 1)
    parity = parity_ref[0]
    for number in range(3):
        wanted = place + (number + parity * (2 - 2 * number)) * BLOCKS
        hits = jnp.concatenate(
            [one_hot(codes[:, s : s + 1], wanted) for s in range(SLOTS)], axis=0
        )
        counts_ref[number] = dot(chosen, hits).astype(BF16)


def eval_tables(rows_ref, cols_ref, left_ref, right_high_ref, right_low_ref):
    harmonics, side = rows_ref.shape
    rows = jnp.concatenate([rows_ref[...]] * 4, axis=0)
    rows = jnp.where(
        lax.broadcasted_iota(jnp.int32, rows.shape, 0) // harmonics
        == lax.broadcasted_iota(jnp.int32, rows.shape, 1) // (side // 4),
        rows,
        0.0,
    )
    high, low = halves(rows.T)
    left_ref[...] = jnp.concatenate([high, high, low, low], axis=1)
    for ref, part in zip((right_high_ref, right_low_ref), halves(cols_ref[...])):
        ref[...] = jnp.zeros_like(ref)
        for row in range(harmonics):
            ref[row * harmonics : (row + 1) * harmonics, row * side : (row + 1) * side] = part


def column_of(ref):
    side = ref.shape[0]
    leaf = lax.broadcasted_iota(jnp.int32, (LEAVES, side), 0)
    place = lax.broadcasted_iota(jnp.int32, (LEAVES, side), 1)
    spread = dot(one_hot(leaf // side, place), ref[...].astype(F32).astype(BF16))
    kept = jnp.where(leaf % side == place, spread, 0.0)
    return jnp.sum(kept, axis=1, keepdims=True).astype(jnp.int32)


def ready_kernel(
    parity_ref,
    src_ref,
    kind_ref,
    count_ref,
    density_ref,
    kinds_ref,
    list_ref,
    op_ref,
    rows_ref,
    cols_ref,
    out_ref,
    counts_ref,
    left_ref,
    right_high_ref,
    right_low_ref,
    products,
):
    near_field(src_ref, kind_ref, count_ref, density_ref, kinds_ref, out_ref, products)
    count_tables(parity_ref, list_ref, op_ref, counts_ref)
    eval_tables(rows_ref, cols_ref, left_ref, right_high_ref, right_low_ref)


def parent_kernel(own_ref, gathered_ref, shift_ref, window_ref, parents_ref):
    peers = gathered_ref.shape[0]
    flat = (peers * LEAVES, HALF)
    sources = jnp.concatenate(
        [
            gathered_ref[:, :LEAVES, :].reshape(flat),
            gathered_ref[:, LEAVES : 2 * LEAVES, :].reshape(flat),
        ],
        axis=1,
    )
    labels = []
    for peer in range(peers):
        numbers = gathered_ref[peer, 2 * LEAVES :, :].astype(F32)
        labels.append(numbers[0:1, :LEAVES] + numbers[1:2, :LEAVES] * float(PARENTS))
    labels = jnp.concatenate(labels, axis=1).astype(jnp.int32)
    positions = lax.broadcasted_iota(jnp.int32, (PARENTS, peers * LEAVES), 0)
    ordered = [
        dot(one_hot(labels, positions + octant * PARENTS), sources).astype(BF16)
        for octant in range(OCTANTS)
    ]
    total = jnp.zeros((PARENTS, COEFFS), F32)
    for octant in range(OCTANTS):
        total = total + dot(ordered[octant], shift_ref[octant])
    parents = total.astype(BF16)
    parents_ref[...] = parents
    window_ref[:PARENTS, :] = parents
    own = own_ref[0]
    for place in range(3):
        peer = lax.rem(own + place + peers - 1, peers)
        rows = slice(PARENTS + place * LEAVES, PARENTS + (place + 1) * LEAVES)
        window_ref[rows, :HALF] = gathered_ref[peer, :LEAVES, :]
        window_ref[rows, HALF:] = gathered_ref[peer, LEAVES : 2 * LEAVES, :]


def op_rows(numbers, first, slots):
    rows = [numbers[first + slot : first + slot + 1, :] for slot in range(slots)]
    return jnp.concatenate(rows, axis=1)


def operator_masks(rows, slots):
    shape = (LEAVES, slots * LEAVES)
    same = (lax.broadcasted_iota(jnp.int32, shape, 1) % LEAVES) == lax.broadcasted_iota(
        jnp.int32, shape, 0
    )
    diagonal = jnp.where(same, rows, -1.0)
    return jnp.concatenate([one_hot(diagonal, float(op)) for op in range(OPS)], axis=0)


def pick_table():
    shape = (16, COEFFS)
    row = lax.broadcasted_iota(jnp.int32, shape, 0)
    lane = lax.broadcasted_iota(jnp.int32, shape, 1)
    part, slot = lane // LEAVES, lane % PSLOTS
    value = jnp.where(part == 0, 128.0, 1.0)
    hit = (part < 2) & (row == slot) | (part == 2) & (row == slot + PSLOTS)
    return jnp.where(hit, value, 0.0).astype(BF16)


def coarse_kernel(
    parity_ref,
    parent_ref,
    gathered_ref,
    own_ref,
    counts_ref,
    leaf_ref,
    hits_ref,
    masks_ref,
):
    leaf_ref[...] = dot(counts_ref[1], own_ref[PARENTS:, :])
    peers = gathered_ref.shape[0]
    parent_of = column_of(parent_ref)
    pick = pick_table()
    lists = []
    for peer in range(peers):
        numbers = gathered_ref[peer, 2 * LEAVES :, :].astype(F32)
        lists.append(jnp.concatenate([numbers[2:3], numbers[3:4]], axis=1))
    lists = jnp.concatenate(lists, axis=0).astype(BF16)
    owner = one_hot(parent_of // 8, lax.broadcasted_iota(jnp.int32, (LEAVES, peers), 1))
    entries = dot(owner, lists)
    lane = lax.broadcasted_iota(jnp.int32, (LEAVES, COEFFS), 1)
    entries = jnp.where((lane % LEAVES) // 8 == parent_of % 8, entries, 0.0).astype(BF16)
    by_leaf = dot_rows(entries, pick).astype(jnp.int32)
    by_slot = dot_rows(pick, entries)
    masks_ref[...] = operator_masks(op_rows(by_slot, PSLOTS, PSLOTS), PSLOTS)
    column = lax.broadcasted_iota(jnp.int32, (LEAVES, PARENTS), 1)
    parity = parity_ref[0]
    for number in range(5):
        wanted = column + (number + parity * (4 - 2 * number)) * PARENTS
        hits_ref[:, number * PARENTS : (number + 1) * PARENTS] = jnp.concatenate(
            [one_hot(by_leaf[:, s : s + 1], wanted) for s in range(PSLOTS)], axis=0
        )


def final_kernel(
    octant_ref,
    counts_ref,
    leaf_ref,
    hits_ref,
    masks_ref,
    own_ref,
    near2_ref,
    near1_ref,
    mate_ref,
    far2_ref,
    operators_ref,
    shift_ref,
    left_ref,
    right_high_ref,
    right_low_ref,
    near_ref,
    out_ref,
    staged,
):
    leaf_sums = (
        leaf_ref[...]
        + dot(counts_ref[0], near1_ref[PARENTS:, :])
        + dot(counts_ref[2], mate_ref[PARENTS:, :])
    )
    sources = jnp.concatenate(
        [
            near2_ref[...],
            near1_ref[:PARENTS, :],
            own_ref[:PARENTS, :],
            mate_ref[:PARENTS, :],
            far2_ref[...],
        ],
        axis=0,
    )
    coarse_sums = dot(masks_ref[...], dot(hits_ref[...], sources).astype(BF16))
    leaf_high, leaf_low = halves(leaf_sums)
    coarse_high, coarse_low = halves(coarse_sums)
    total = jnp.zeros((4 * LEAVES, COEFFS), F32)
    for op in range(OPS):
        rows = slice(op * LEAVES, (op + 1) * LEAVES)
        stacked = jnp.concatenate(
            [leaf_high[rows], leaf_low[rows], coarse_high[rows], coarse_low[rows]], axis=0
        )
        total = total + dot(stacked, operators_ref[op])
    local = total[:LEAVES] + total[LEAVES : 2 * LEAVES]
    coarse_local = total[2 * LEAVES : 3 * LEAVES] + total[3 * LEAVES :]
    coarse_local = coarse_local.astype(BF16).astype(F32)
    octant_of = column_of(octant_ref)
    for octant in range(OCTANTS):
        chosen = jnp.where(octant_of == octant, coarse_local, 0.0).astype(BF16)
        local = local + dot_rows(chosen, shift_ref[octant])

    high, low = halves(local)
    spread = dot(jnp.concatenate([high, low], axis=0), right_high_ref[...])
    spread = spread[:LEAVES] + spread[LEAVES:] + dot(high, right_low_ref[...])
    harmonics = 16
    side = out_ref.shape[1]
    for row in range(harmonics):
        staged[pl.ds(row, LEAVES, stride=harmonics), :] = spread[:, row * side : (row + 1) * side]
    left = left_ref[...]
    for pair in range(out_ref.shape[0] // 2):
        parts = []
        for tile in (2 * pair, 2 * pair + 1):
            tile_high, tile_low = halves(staged[tile * LEAVES : (tile + 1) * LEAVES, :])
            parts.append(jnp.concatenate([tile_high, tile_low, tile_high, tile_low], axis=0))
        far = dot(left, jnp.concatenate(parts, axis=1))
        for half, tile in enumerate((2 * pair, 2 * pair + 1)):
            out_ref[tile] = (near_ref[tile] + far[:, half * side : (half + 1) * side]).astype(BF16)


VMEM = pl.BlockSpec(memory_space=pltpu.VMEM)
SMEM = pl.BlockSpec(memory_space=pltpu.SMEM)
HBM = pl.BlockSpec(memory_space=pltpu.HBM)


def ready_call(*operands):
    density, kinds = operands[4:6]
    tiles, side, _ = density.shape
    right = jax.ShapeDtypeStruct((COEFFS, 16 * side), BF16)
    return pl.pallas_call(
        ready_kernel,
        name="ready",
        out_shape=(
            jax.ShapeDtypeStruct((tiles, side, side), F32),
            jax.ShapeDtypeStruct((3, OPS * LEAVES, BLOCKS), BF16),
            jax.ShapeDtypeStruct((side, 4 * LEAVES), BF16),
            right,
            right,
        ),
        in_specs=[SMEM] * 4 + [VMEM] * 6,
        out_specs=(VMEM,) * 5,
        scratch_shapes=[pltpu.VMEM((tiles, kinds.shape[0], side, side), F32)],
        compiler_params=pltpu.CompilerParams(vmem_limit_bytes=67043328 - 4 * MIB // 2),
        cost_estimate=pl.CostEstimate(
            flops=8 * 10**9, bytes_accessed=6 * MIB, transcendentals=0
        ),
    )(*operands)


def payload_call(peers, *operands):
    return pl.pallas_call(
        payload_kernel,
        name="payload",
        out_shape=jax.ShapeDtypeStruct((peers, ROWS, HALF), BF16),
        in_specs=[HBM] * len(operands),
        out_specs=HBM,
        scratch_shapes=[pltpu.VMEM(operand.shape, operand.dtype) for operand in operands]
        + [
            pltpu.VMEM((ROWS, HALF), BF16),
            pltpu.SemaphoreType.DMA((len(operands),)),
            pltpu.SemaphoreType.DMA((2, peers)),
        ],
        compiler_params=pltpu.CompilerParams(vmem_limit_bytes=67043328),
        cost_estimate=pl.CostEstimate(
            flops=10**9, bytes_accessed=MIB, transcendentals=0
        ),
    )(*operands)


def parent_call(own, gathered, shift_up):
    return pl.pallas_call(
        parent_kernel,
        name="parents",
        out_shape=(
            jax.ShapeDtypeStruct((PARENTS + BLOCKS, COEFFS), BF16),
            jax.ShapeDtypeStruct((PARENTS, COEFFS), BF16),
        ),
        in_specs=[SMEM, VMEM, VMEM],
        out_specs=(VMEM, VMEM),
        compiler_params=pltpu.CompilerParams(vmem_limit_bytes=12 * MIB),
        cost_estimate=pl.CostEstimate(
            flops=2 * 10**9, bytes_accessed=2 * MIB, transcendentals=0
        ),
    )(own, gathered, shift_up)


def coarse_call(*operands):
    rows = OPS * LEAVES
    return pl.pallas_call(
        coarse_kernel,
        name="coarse",
        out_shape=(
            jax.ShapeDtypeStruct((rows, COEFFS), F32),
            jax.ShapeDtypeStruct((PSLOTS * LEAVES, 5 * PARENTS), BF16),
            jax.ShapeDtypeStruct((rows, PSLOTS * LEAVES), BF16),
        ),
        in_specs=[SMEM] + [VMEM] * (len(operands) - 1),
        out_specs=(VMEM, VMEM, VMEM),
        compiler_params=pltpu.CompilerParams(vmem_limit_bytes=16 * MIB),
        cost_estimate=pl.CostEstimate(
            flops=1000000000, bytes_accessed=4 * MIB, transcendentals=0
        ),
    )(*operands)


def final_call(*operands):
    near = operands[-1]
    return pl.pallas_call(
        final_kernel,
        name="final",
        out_shape=jax.ShapeDtypeStruct(near.shape, BF16),
        in_specs=[VMEM] * len(operands),
        out_specs=VMEM,
        scratch_shapes=[pltpu.VMEM((LEAVES * 16, near.shape[1]), F32)],
        compiler_params=pltpu.CompilerParams(vmem_limit_bytes=20 * MIB),
        cost_estimate=pl.CostEstimate(
            flops=4 * 10**9, bytes_accessed=8 * MIB, transcendentals=0
        ),
    )(*operands)


def routed(value, axis, to_even, to_odd):
    peers = lax.axis_size(axis)
    route = [(i, (i + (to_odd if i % 2 else to_even)) % peers) for i in range(peers)]
    return lax.ppermute(value, axis, route)


def body(
    leaf_moments,
    leaf_list,
    leaf_op,
    leaf_parent,
    leaf_octant,
    parent_list,
    parent_op,
    operators,
    shift_up,
    density,
    nearby_coulomb_kernel,
    near_src,
    near_kind,
    near_count,
    eval_rows,
    eval_cols,
):
    own = lax.axis_index("yz").astype(jnp.int32).reshape(1)
    parity = (lax.axis_index("gx") % 2).astype(jnp.int32).reshape(1)
    sent = payload_call(
        lax.axis_size("yz"),
        leaf_moments.reshape(LEAVES, COEFFS),
        leaf_parent,
        leaf_octant,
        parent_list[0],
        parent_op[0],
    )
    gathered = lax.all_to_all(sent, "yz", split_axis=0, concat_axis=0, tiled=True)

    near, counts, left, right_high, right_low = ready_call(
        parity,
        near_src,
        near_kind,
        near_count,
        density,
        nearby_coulomb_kernel,
        leaf_list.reshape(LEAVES, SLOTS),
        leaf_op.reshape(LEAVES, SLOTS),
        eval_rows.T,
        eval_cols,
    )

    window, parents = parent_call(own, gathered, shift_up)
    near1 = routed(window, "gx", -1, 1)
    near2 = routed(parents, "gx", 2, -2)
    far2 = routed(parents, "gx", -2, 2)
    mate = routed(window, "gx", 1, -1)
    leaf, hits, masks = coarse_call(
        parity, leaf_parent, gathered, window, counts
    )
    return final_call(
        leaf_octant,
        counts,
        leaf,
        hits,
        masks,
        window,
        near2,
        near1,
        mate,
        far2,
        operators,
        shift_up,
        left,
        right_high,
        right_low,
        near,
    )


def solution(mesh):
    in_specs = (
        P("gx", "yz", None),
        P("gx", "yz", None),
        P("gx", "yz", None),
        P("gx", "yz"),
        P("gx", "yz"),
        P("gx", "yz", None),
        P("gx", "yz", None),
        P(),
        P(),
        P(("gx", "yz"), None, None),
        P(),
        P(("gx", "yz"), None),
        P(("gx", "yz"), None),
        P(("gx", "yz")),
        P(),
        P(),
    )
    out_specs = P(("gx", "yz"), None, None)
    return jax.shard_map(body, mesh=mesh, in_specs=in_specs, out_specs=out_specs, check_vma=False)
```

profile of v0, /device:TPU:1, one launch (start us, length us, event | category | flops | bytes accessed | tf_op | source)
XLA Modules:
  0.0 73.9 jit_solution(13631585010033658027)
XLA Ops:
  0.0 2.0 %payload.1 = bf16[16,136,128]{2,1,0:T(8,128)(2,1)} custom-call(bf16[64,256]{1,0:T(8,128)(2,1)} %bitcast.8, s32[8,8]{1,0:T(8,128)} %parent_ref.1, s32[8,8]{1,0:T(8,128)} %octant_ref.1, s32[8,8]{1,0:T(8,128)} %bitcast.12, s32[8,8]{1,0:T(8,128)} %bitcast.13), custom_call_target="tpu_custom_call" | custom-call | flops 1000000000 | bytes 1048576 | tf_op jit(solution)/shard_map/payload/pallas_call | solution.py:393
  2.0 10.2 %all-to-all-start = ((bf16[16,136,128]{2,1,0:T(8,128)(2,1)}), bf16[16,136,128]{2,1,0:T(8,128)(2,1)S(1)}, u32[]{:S(2)}, u32[]{:S(2)}) async-start(bf16[16,136,128]{2,1,0:T(8,128)(2,1)} %payload.1), calls=%async_computation | async-start | bytes 1114112 | tf_op jit(solution)/shard_map/all_to_all | solution.py:498
  12.2 16.1 %all-to-all-done.gathered_ref = bf16[16,136,128]{2,1,0:T(8,128)(2,1)S(1)} async-done(((bf16[16,136,128]{2,1,0:T(8,128)(2,1)}), bf16[16,136,128]{2,1,0:T(8,128)(2,1)S(1)}, u32[]{:S(2)}, u32[]{:S(2)}) %all-to-all-start) | async-done | bytes 557088 | tf_op jit(solution)/shard_map/all_to_all | solution.py:498
  28.3 0.0 copy-start.1
  28.3 1.2 %copy-done.1 = bf16[8,256,256]{2,1,0:T(8,128)(2,1)S(1)} copy-done((bf16[8,256,256]{2,1,0:T(8,128)(2,1)S(1)}, bf16[8,256,256]{2,1,0:T(8,128)(2,1)}, u32[]{:S(2)}) %copy-start.1) | copy-done | bytes 1048600
  29.5 1.0 %parents.1 = (bf16[320,256]{1,0:T(8,128)(2,1)S(1)}, bf16[128,256]{1,0:T(8,128)(2,1)S(1)}) custom-call(s32[1]{0:T(128)} %bitcast.7.own_ref, bf16[16,136,128]{2,1,0:T(8,128)(2,1)S(1)} %all-to-all-done.gathered_ref, bf16[8,256,256]{2,1,0:T(8,128)(2,1)S(1)} %copy-done.1), custom_call_target="tpu_custom_call" | custom-call | flops 2000000000 | bytes 2097152 | tf_op jit(solution)/shard_map/parents/pallas_call | solution.py:413
  30.5 6.6 %collective-permute-start.1 = (bf16[320,256]{1,0:T(8,128)(2,1)S(1)}, bf16[320,256]{1,0:T(8,128)(2,1)S(1)}, u32[]{:S(2)}, u32[]{:S(2)}) collective-permute-start(bf16[320,256]{1,0:T(8,128)(2,1)S(1)} %get-tuple-element.16.own_ref), channel_id=1, source_target_pairs={{0,496},{16,32},{32,16},{48,64},{64,48},{80,96},{96,80},{112,128},... | collective-permute-start | bytes 491528 | tf_op jit(solution)/shard_map/ppermute | solution.py:467
  37.1 6.4 %collective-permute-start.2 = (bf16[320,256]{1,0:T(8,128)(2,1)S(1)}, bf16[320,256]{1,0:T(8,128)(2,1)S(1)}, u32[]{:S(2)}, u32[]{:S(2)}) collective-permute-start(bf16[320,256]{1,0:T(8,128)(2,1)S(1)} %get-tuple-element.16.own_ref), channel_id=1, source_target_pairs={{0,16},{16,0},{32,48},{48,32},{64,80},{80,64},{96,112},{112,96},{1... | collective-permute-start | bytes 491528 | tf_op jit(solution)/shard_map/ppermute | solution.py:467
  43.5 0.0 copy-start.3
  43.5 9.3 %ready.1 = (f32[16,128,128]{2,1,0:T(8,128)}, bf16[3,1024,192]{2,1,0:T(8,128)(2,1)}, bf16[128,256]{1,0:T(8,128)(2,1)}, bf16[256,2048]{1,0:T(8,128)(2,1)}, bf16[256,2048]{1,0:T(8,128)(2,1)}) custom-call(s32[1]{0:T(128)} %bitcast.parity_ref, s32[16,16]{1,0:T(8,128)} %src_ref.1, s32[16,16]{1,0:T(8,128)} %kind_ref.1, s32[16]{0:T(128)} %count_ref.1, ...), custom_call_target="tpu_custom_call" | custom-call | flops 8000000000 | bytes 6291456 | tf_op jit(solution)/shard_map/ready/pallas_call | solution.py:372
  52.9 0.0 copy-start
  52.9 0.0 copy-start.2
  52.9 0.0 copy-start.4
  52.9 4.0 %collective-permute-start = (bf16[128,256]{1,0:T(8,128)(2,1)S(1)}, bf16[128,256]{1,0:T(8,128)(2,1)S(1)}, u32[]{:S(2)}, u32[]{:S(2)}) collective-permute-start(bf16[128,256]{1,0:T(8,128)(2,1)S(1)} %get-tuple-element.20), channel_id=1, source_target_pairs={{0,32},{16,496},{32,64},{48,16},{64,96},{80,48},{96,128},{112,80},... | collective-permute-start | bytes 196616 | tf_op jit(solution)/shard_map/ppermute | solution.py:467
  56.9 1.9 %collective-permute-start.3 = (bf16[128,256]{1,0:T(8,128)(2,1)S(1)}, bf16[128,256]{1,0:T(8,128)(2,1)S(1)}, u32[]{:S(2)}, u32[]{:S(2)}) collective-permute-start(bf16[128,256]{1,0:T(8,128)(2,1)S(1)} %get-tuple-element.20), channel_id=1, source_target_pairs={{0,480},{16,48},{32,0},{48,80},{64,32},{80,112},{96,64},{112,144},... | collective-permute-start | bytes 196616 | tf_op jit(solution)/shard_map/ppermute | solution.py:467
  58.8 0.0 copy-done.3
  58.8 0.0 copy-start.5
  58.8 1.4 %copy-done.5 = bf16[3,1024,192]{2,1,0:T(8,128)(2,1)S(1)} copy-done((bf16[3,1024,192]{2,1,0:T(8,128)(2,1)S(1)}, bf16[3,1024,192]{2,1,0:T(8,128)(2,1)}, u32[]{:S(2)}) %copy-start.5) | copy-done | bytes 1179672
  60.2 0.0 copy-start.10
  60.2 1.0 %coarse.1 = (f32[1024,256]{1,0:T(8,128)S(1)}, bf16[512,640]{1,0:T(8,128)(2,1)S(1)}, bf16[1024,512]{1,0:T(8,128)(2,1)S(1)}) custom-call(s32[1]{0:T(128)} %bitcast.parity_ref, s32[8,8]{1,0:T(8,128)S(1)} %copy-done.3, bf16[16,136,128]{2,1,0:T(8,128)(2,1)S(1)} %all-to-all-done.gathered_ref, bf16[320,256]{1,0:T(8,128)(2,1)S(1)} %get-tuple-element.16.own_ref, ...), custom_call_target="tpu_custom_call" | custom-call | flops 1000000000 | bytes 4194304 | tf_op jit(solution)/shard_map/coarse/pallas_call | solution.py:431
  61.3 0.0 collective-permute-done.near2_ref
  61.3 2.7 %collective-permute-done.3.far2_ref = bf16[128,256]{1,0:T(8,128)(2,1)S(1)} collective-permute-done((bf16[128,256]{1,0:T(8,128)(2,1)S(1)}, bf16[128,256]{1,0:T(8,128)(2,1)S(1)}, u32[]{:S(2)}, u32[]{:S(2)}) %collective-permute-start.3) | collective-permute-done | bytes 65568 | tf_op jit(solution)/shard_map/ppermute | solution.py:467
  64.0 0.0 collective-permute-done.1.near1_ref
  64.0 0.0 collective-permute-done.2.mate_ref
  64.0 0.0 copy-done
  64.0 0.0 copy-done.2
  64.0 0.0 copy-done.4
  64.0 0.0 copy-done.10
  64.1 0.0 copy-start.6
  64.1 1.4 %copy-done.6 = bf16[3,1024,192]{2,1,0:T(8,128)(2,1)S(1)} copy-done((bf16[3,1024,192]{2,1,0:T(8,128)(2,1)S(1)}, bf16[3,1024,192]{2,1,0:T(8,128)(2,1)}, u32[]{:S(2)}) %copy-start.6) | copy-done | bytes 1179672
  65.5 0.0 copy-start.7
  65.5 1.2 %copy-done.7 = f32[16,128,128]{2,1,0:T(8,128)S(1)} copy-done((f32[16,128,128]{2,1,0:T(8,128)S(1)}, f32[16,128,128]{2,1,0:T(8,128)}, u32[]{:S(2)}) %copy-start.7) | copy-done | bytes 1048600
  66.7 0.0 copy-start.8
  66.7 1.2 %copy-done.8 = bf16[256,2048]{1,0:T(8,128)(2,1)S(1)} copy-done((bf16[256,2048]{1,0:T(8,128)(2,1)S(1)}, bf16[256,2048]{1,0:T(8,128)(2,1)}, u32[]{:S(2)}) %copy-start.8) | copy-done | bytes 1048600
  67.9 0.0 copy-start.9
  67.9 1.2 %copy-done.9 = bf16[256,2048]{1,0:T(8,128)(2,1)S(1)} copy-done((bf16[256,2048]{1,0:T(8,128)(2,1)S(1)}, bf16[256,2048]{1,0:T(8,128)(2,1)}, u32[]{:S(2)}) %copy-start.9) | copy-done | bytes 1048600
  69.1 4.7 %final.1 = bf16[16,128,128]{2,1,0:T(8,128)(2,1)} custom-call(s32[8,8]{1,0:T(8,128)S(1)} %copy-done.4, bf16[3,1024,192]{2,1,0:T(8,128)(2,1)S(1)} %copy-done.6, f32[1024,256]{1,0:T(8,128)S(1)} %get-tuple-element.17.leaf_ref, bf16[512,640]{1,0:T(8,128)(2,1)S(1)} %get-tuple-element.18.hits_ref, bf16[1024,512]{1,0:T(8,128)(2,1)S(1)} %get-tuple-element.19.masks_ref, ...), custom_call_target="tpu_custom_call" | custom-call | flops 4000000000 | bytes 8388608 | tf_op jit(solution)/shard_map/final/pallas_call | solution.py:450
Async XLA Ops:
  2.0 26.3 %all-to-all-start = ((bf16[16,136,128]{2,1,0:T(8,128)(2,1)}), bf16[16,136,128]{2,1,0:T(8,128)(2,1)S(1)}, u32[]{:S(2)}, u32[]{:S(2)}) async-start(bf16[16,136,128]{2,1,0:T(8,128)(2,1)} %payload.1), calls=%async_computation | async-start | bytes 1114112 | tf_op jit(solution)/shard_map/all_to_all | solution.py:498
  28.3 1.2 %copy-start.1 = (bf16[8,256,256]{2,1,0:T(8,128)(2,1)S(1)}, bf16[8,256,256]{2,1,0:T(8,128)(2,1)}, u32[]{:S(2)}) copy-start(bf16[8,256,256]{2,1,0:T(8,128)(2,1)} %shift_ref.3) | copy-start | bytes 3145732
  30.5 33.5 %collective-permute-start.1 = (bf16[320,256]{1,0:T(8,128)(2,1)S(1)}, bf16[320,256]{1,0:T(8,128)(2,1)S(1)}, u32[]{:S(2)}, u32[]{:S(2)}) collective-permute-start(bf16[320,256]{1,0:T(8,128)(2,1)S(1)} %get-tuple-element.16.own_ref), channel_id=1, source_target_pairs={{0,496},{16,32},{32,16},{48,64},{64,48},{80,96},{96,80},{112,128},... | collective-permute-start | bytes 491528 | tf_op jit(solution)/shard_map/ppermute | solution.py:467
  37.1 26.9 %collective-permute-start.2 = (bf16[320,256]{1,0:T(8,128)(2,1)S(1)}, bf16[320,256]{1,0:T(8,128)(2,1)S(1)}, u32[]{:S(2)}, u32[]{:S(2)}) collective-permute-start(bf16[320,256]{1,0:T(8,128)(2,1)S(1)} %get-tuple-element.16.own_ref), channel_id=1, source_target_pairs={{0,16},{16,0},{32,48},{48,32},{64,80},{80,64},{96,112},{112,96},{1... | collective-permute-start | bytes 491528 | tf_op jit(solution)/shard_map/ppermute | solution.py:467
  43.5 15.3 %copy-start.3 = (s32[8,8]{1,0:T(8,128)S(1)}, s32[8,8]{1,0:T(8,128)}, u32[]{:S(2)}) copy-start(s32[8,8]{1,0:T(8,128)} %parent_ref.1) | copy-start | bytes 772
  52.9 11.1 %copy-start = (bf16[16,256,256]{2,1,0:T(8,128)(2,1)S(1)}, bf16[16,256,256]{2,1,0:T(8,128)(2,1)}, u32[]{:S(2)}) copy-start(bf16[16,256,256]{2,1,0:T(8,128)(2,1)} %operators_ref.1) | copy-start | bytes 6291460
  52.9 11.2 %copy-start.2 = (bf16[8,256,256]{2,1,0:T(8,128)(2,1)S(1)}, bf16[8,256,256]{2,1,0:T(8,128)(2,1)}, u32[]{:S(2)}) copy-start(bf16[8,256,256]{2,1,0:T(8,128)(2,1)} %shift_ref.3) | copy-start | bytes 3145732
  52.9 11.2 %copy-start.4 = (s32[8,8]{1,0:T(8,128)S(1)}, s32[8,8]{1,0:T(8,128)}, u32[]{:S(2)}) copy-start(s32[8,8]{1,0:T(8,128)} %octant_ref.1) | copy-start | bytes 772
  52.9 8.4 %collective-permute-start = (bf16[128,256]{1,0:T(8,128)(2,1)S(1)}, bf16[128,256]{1,0:T(8,128)(2,1)S(1)}, u32[]{:S(2)}, u32[]{:S(2)}) collective-permute-start(bf16[128,256]{1,0:T(8,128)(2,1)S(1)} %get-tuple-element.20), channel_id=1, source_target_pairs={{0,32},{16,496},{32,64},{48,16},{64,96},{80,48},{96,128},{112,80},... | collective-permute-start | bytes 196616 | tf_op jit(solution)/shard_map/ppermute | solution.py:467
  56.9 7.1 %collective-permute-start.3 = (bf16[128,256]{1,0:T(8,128)(2,1)S(1)}, bf16[128,256]{1,0:T(8,128)(2,1)S(1)}, u32[]{:S(2)}, u32[]{:S(2)}) collective-permute-start(bf16[128,256]{1,0:T(8,128)(2,1)S(1)} %get-tuple-element.20), channel_id=1, source_target_pairs={{0,480},{16,48},{32,0},{48,80},{64,32},{80,112},{96,64},{112,144},... | collective-permute-start | bytes 196616 | tf_op jit(solution)/shard_map/ppermute | solution.py:467
  58.8 1.4 %copy-start.5 = (bf16[3,1024,192]{2,1,0:T(8,128)(2,1)S(1)}, bf16[3,1024,192]{2,1,0:T(8,128)(2,1)}, u32[]{:S(2)}) copy-start(bf16[3,1024,192]{2,1,0:T(8,128)(2,1)} %get-tuple-element.15.counts_ref) | copy-start | bytes 3538948
  60.2 3.8 %copy-start.10 = (bf16[128,256]{1,0:T(8,128)(2,1)S(1)}, bf16[128,256]{1,0:T(8,128)(2,1)}, u32[]{:S(2)}) copy-start(bf16[128,256]{1,0:T(8,128)(2,1)} %get-tuple-element.21.left_ref) | copy-start | bytes 196612
  64.1 1.4 %copy-start.6 = (bf16[3,1024,192]{2,1,0:T(8,128)(2,1)S(1)}, bf16[3,1024,192]{2,1,0:T(8,128)(2,1)}, u32[]{:S(2)}) copy-start(bf16[3,1024,192]{2,1,0:T(8,128)(2,1)} %get-tuple-element.15.counts_ref) | copy-start | bytes 3538948
  65.5 1.2 %copy-start.7 = (f32[16,128,128]{2,1,0:T(8,128)S(1)}, f32[16,128,128]{2,1,0:T(8,128)}, u32[]{:S(2)}) copy-start(f32[16,128,128]{2,1,0:T(8,128)} %get-tuple-element.24.near_ref) | copy-start | bytes 3145732
  66.7 1.2 %copy-start.8 = (bf16[256,2048]{1,0:T(8,128)(2,1)S(1)}, bf16[256,2048]{1,0:T(8,128)(2,1)}, u32[]{:S(2)}) copy-start(bf16[256,2048]{1,0:T(8,128)(2,1)} %get-tuple-element.22.right_high_ref) | copy-start | bytes 3145732
  67.9 1.2 %copy-start.9 = (bf16[256,2048]{1,0:T(8,128)(2,1)S(1)}, bf16[256,2048]{1,0:T(8,128)(2,1)}, u32[]{:S(2)}) copy-start(bf16[256,2048]{1,0:T(8,128)(2,1)} %get-tuple-element.23.right_low_ref) | copy-start | bytes 3145732
where the time goes:
time: 74.4 us; the launch traced here: 73.9 us
  starting transfers between devices  29.1 us (39%)
  waiting for transfers between devices  18.8 us (25%)
  Pallas kernels  18 us (24%)
  local copies, waits for them, and re-layouts  7.72 us (10%)
    ppermute x4, starting transfers between devices, routed(): return lax.ppermute(value, axis, route)  18.9 us
    all_to_all x1, waiting for transfers between devices, body(): lax.all_to_all(sent, 'yz', split_axis=0, concat_axis=0, tiled=True)  16.1 us
    all_to_all x1, starting transfers between devices, body(): lax.all_to_all(sent, 'yz', split_axis=0, concat_axis=0, tiled=True)  10.2 us
    pallas_call x1, Pallas kernels, ready_call(): pl.pallas_call(ready_kernel, name='ready', out_shape=(jax.ShapeDtypeStruc...  9.34 us
    unnamed x22, local copies, waits for them, and re-layouts  7.72 us
    pallas_call x1, Pallas kernels, final_call(): pl.pallas_call(final_kernel, name='final', out_shape=jax.ShapeDtypeStruct...  4.71 us
    ppermute x4, waiting for transfers between devices, routed(): return lax.ppermute(value, axis, route)  2.74 us
    pallas_call x1, Pallas kernels, payload_call(): pl.pallas_call(payload_kernel, name='payload', out_shape=jax.ShapeDtypeSt...  1.96 us
  transfers between devices with their start and end apart: 5, of which 2 were waited for; matrix products, arithmetic and copies ran while one was open for 0% of the time, Pallas kernels for 14%

commit v1 on v0

--- a/solution.py
+++ b/solution.py
@@ -147,7 +147,7 @@
         counts_ref[number] = dot(chosen, hits).astype(BF16)
 
 
-def eval_tables(rows_ref, cols_ref, left_ref, right_high_ref, right_low_ref):
+def eval_tables(rows_ref, cols_ref, left_ref, right_ref):
     harmonics, side = rows_ref.shape
     rows = jnp.concatenate([rows_ref[...]] * 4, axis=0)
     rows = jnp.where(
@@ -158,10 +158,11 @@
     )
     high, low = halves(rows.T)
     left_ref[...] = jnp.concatenate([high, high, low, low], axis=1)
-    for ref, part in zip((right_high_ref, right_low_ref), halves(cols_ref[...])):
-        ref[...] = jnp.zeros_like(ref)
-        for row in range(harmonics):
-            ref[row * harmonics : (row + 1) * harmonics, row * side : (row + 1) * side] = part
+    high, low = halves(cols_ref[...])
+    right_ref[...] = jnp.zeros_like(right_ref)
+    right_ref[:harmonics, :side] = high
+    right_ref[:harmonics, side:] = low
+    right_ref[side : side + harmonics, :side] = high
 
 
 def column_of(ref):
@@ -187,13 +188,12 @@
     out_ref,
     counts_ref,
     left_ref,
-    right_high_ref,
-    right_low_ref,
+    right_ref,
     products,
 ):
     near_field(src_ref, kind_ref, count_ref, density_ref, kinds_ref, out_ref, products)
     count_tables(parity_ref, list_ref, op_ref, counts_ref)
-    eval_tables(rows_ref, cols_ref, left_ref, right_high_ref, right_low_ref)
+    eval_tables(rows_ref, cols_ref, left_ref, right_ref)
 
 
 def parent_kernel(own_ref, gathered_ref, shift_ref, window_ref, parents_ref):
@@ -303,8 +303,7 @@
     operators_ref,
     shift_ref,
     left_ref,
-    right_high_ref,
-    right_low_ref,
+    right_ref,
     near_ref,
     out_ref,
     staged,
@@ -342,18 +341,21 @@
         chosen = jnp.where(octant_of == octant, coarse_local, 0.0).astype(BF16)
         local = local + dot_rows(chosen, shift_ref[octant])
 
-    high, low = halves(local)
-    spread = dot(jnp.concatenate([high, low], axis=0), right_high_ref[...])
-    spread = spread[:LEAVES] + spread[LEAVES:] + dot(high, right_low_ref[...])
     harmonics = 16
     side = out_ref.shape[1]
     for row in range(harmonics):
-        staged[pl.ds(row, LEAVES, stride=harmonics), :] = spread[:, row * side : (row + 1) * side]
+        first = row * harmonics
+        block = local[:, first // side * side : first // side * side + side]
+        if first % side:
+            block = pltpu.roll(block, side - first % side, 1)
+        staged[pl.ds(row, LEAVES, stride=harmonics), :] = block
+    spread = dot(jnp.concatenate(halves(staged[...]), axis=1), right_ref[...])
+    spread = spread[:, :side] + spread[:, side:]
     left = left_ref[...]
     for pair in range(out_ref.shape[0] // 2):
         parts = []
         for tile in (2 * pair, 2 * pair + 1):
-            tile_high, tile_low = halves(staged[tile * LEAVES : (tile + 1) * LEAVES, :])
+            tile_high, tile_low = halves(spread[tile * LEAVES : (tile + 1) * LEAVES])
             parts.append(jnp.concatenate([tile_high, tile_low, tile_high, tile_low], axis=0))
         far = dot(left, jnp.concatenate(parts, axis=1))
         for half, tile in enumerate((2 * pair, 2 * pair + 1)):
@@ -368,7 +370,6 @@
 def ready_call(*operands):
     density, kinds = operands[4:6]
     tiles, side, _ = density.shape
-    right = jax.ShapeDtypeStruct((COEFFS, 16 * side), BF16)
     return pl.pallas_call(
         ready_kernel,
         name="ready",
@@ -376,11 +377,10 @@
             jax.ShapeDtypeStruct((tiles, side, side), F32),
             jax.ShapeDtypeStruct((3, OPS * LEAVES, BLOCKS), BF16),
             jax.ShapeDtypeStruct((side, 4 * LEAVES), BF16),
-            right,
-            right,
+            jax.ShapeDtypeStruct((2 * side, 2 * side), BF16),
         ),
         in_specs=[SMEM] * 4 + [VMEM] * 6,
-        out_specs=(VMEM,) * 5,
+        out_specs=(VMEM,) * 4,
         scratch_shapes=[pltpu.VMEM((tiles, kinds.shape[0], side, side), F32)],
         compiler_params=pltpu.CompilerParams(vmem_limit_bytes=67043328 - 4 * MIB // 2),
         cost_estimate=pl.CostEstimate(
@@ -497,7 +497,7 @@
     )
     gathered = lax.all_to_all(sent, "yz", split_axis=0, concat_axis=0, tiled=True)
 
-    near, counts, left, right_high, right_low = ready_call(
+    near, counts, left, right = ready_call(
         parity,
         near_src,
         near_kind,
@@ -512,8 +512,8 @@
 
     window, parents = parent_call(own, gathered, shift_up)
     near1 = routed(window, "gx", -1, 1)
+    far2 = routed(parents, "gx", -2, 2)
     near2 = routed(parents, "gx", 2, -2)
-    far2 = routed(parents, "gx", -2, 2)
     mate = routed(window, "gx", 1, -1)
     leaf, hits, masks = coarse_call(
         parity, leaf_parent, gathered, window, counts
@@ -532,8 +532,7 @@
         operators,
         shift_up,
         left,
-        right_high,
-        right_low,
+        right,
         near,
     )
 

time: 74.4 us -> 71.1 us (0.956)
  local copies, waits for them, and re-layouts: 7.72 us -> 5.28 us
  Pallas kernels: 18 us -> 17.2 us
    unnamed x22 -> x20, local copies, waits for them, and re-layouts: 7.72 us -> 5.28 us
where the time goes in v1:
time: 71.1 us; the launch traced here: 70.6 us
  starting transfers between devices  29.1 us (41%)
  waiting for transfers between devices  18.8 us (26%)
  Pallas kernels  17.2 us (24%)
  local copies, waits for them, and re-layouts  5.28 us (7%)
    ppermute x4, starting transfers between devices, routed(): return lax.ppermute(value, axis, route)  18.9 us
    all_to_all x1, waiting for transfers between devices, body(): lax.all_to_all(sent, 'yz', split_axis=0, concat_axis=0, tiled=True)  16.1 us
    all_to_all x1, starting transfers between devices, body(): lax.all_to_all(sent, 'yz', split_axis=0, concat_axis=0, tiled=True)  10.2 us
    pallas_call x1, Pallas kernels, ready_call(): pl.pallas_call(ready_kernel, name='ready', out_shape=(jax.ShapeDtypeStruc...  8.79 us
    unnamed x20, local copies, waits for them, and re-layouts  5.28 us
    pallas_call x1, Pallas kernels, final_call(): pl.pallas_call(final_kernel, name='final', out_shape=jax.ShapeDtypeStruct...  4.45 us
    ppermute x4, waiting for transfers between devices, routed(): return lax.ppermute(value, axis, route)  2.74 us
    pallas_call x1, Pallas kernels, payload_call(): pl.pallas_call(payload_kernel, name='payload', out_shape=jax.ShapeDtypeSt...  1.95 us
  transfers between devices with their start and end apart: 5, of which 2 were waited for; matrix products, arithmetic and copies ran while one was open for 0% of the time, Pallas kernels for 14%

profile of v1, /device:TPU:1, one launch (start us, length us, event | category | flops | bytes accessed | tf_op | source)
XLA Modules:
  0.0 70.6 jit_solution(9481676947283412839)
XLA Ops:
  0.0 2.0 %payload.1 = bf16[16,136,128]{2,1,0:T(8,128)(2,1)} custom-call(bf16[64,256]{1,0:T(8,128)(2,1)} %bitcast.8, s32[8,8]{1,0:T(8,128)} %parent_ref.1, s32[8,8]{1,0:T(8,128)} %octant_ref.1, s32[8,8]{1,0:T(8,128)} %bitcast.12, s32[8,8]{1,0:T(8,128)} %bitcast.13), custom_call_target="tpu_custom_call" | custom-call | flops 1000000000 | bytes 1048576 | tf_op jit(solution)/shard_map/payload/pallas_call | solution.py:393
  2.0 10.2 %all-to-all-start = ((bf16[16,136,128]{2,1,0:T(8,128)(2,1)}), bf16[16,136,128]{2,1,0:T(8,128)(2,1)S(1)}, u32[]{:S(2)}, u32[]{:S(2)}) async-start(bf16[16,136,128]{2,1,0:T(8,128)(2,1)} %payload.1), calls=%async_computation | async-start | bytes 1114112 | tf_op jit(solution)/shard_map/all_to_all | solution.py:498
  12.2 16.1 %all-to-all-done.gathered_ref = bf16[16,136,128]{2,1,0:T(8,128)(2,1)S(1)} async-done(((bf16[16,136,128]{2,1,0:T(8,128)(2,1)}), bf16[16,136,128]{2,1,0:T(8,128)(2,1)S(1)}, u32[]{:S(2)}, u32[]{:S(2)}) %all-to-all-start) | async-done | bytes 557088 | tf_op jit(solution)/shard_map/all_to_all | solution.py:498
  28.3 0.0 copy-start.1
  28.3 1.2 %copy-done.1 = bf16[8,256,256]{2,1,0:T(8,128)(2,1)S(1)} copy-done((bf16[8,256,256]{2,1,0:T(8,128)(2,1)S(1)}, bf16[8,256,256]{2,1,0:T(8,128)(2,1)}, u32[]{:S(2)}) %copy-start.1) | copy-done | bytes 1048600
  29.5 1.0 %parents.1 = (bf16[320,256]{1,0:T(8,128)(2,1)S(1)}, bf16[128,256]{1,0:T(8,128)(2,1)S(1)}) custom-call(s32[1]{0:T(128)} %bitcast.7.own_ref, bf16[16,136,128]{2,1,0:T(8,128)(2,1)S(1)} %all-to-all-done.gathered_ref, bf16[8,256,256]{2,1,0:T(8,128)(2,1)S(1)} %copy-done.1), custom_call_target="tpu_custom_call" | custom-call | flops 2000000000 | bytes 2097152 | tf_op jit(solution)/shard_map/parents/pallas_call | solution.py:413
  30.5 6.6 %collective-permute-start.1 = (bf16[320,256]{1,0:T(8,128)(2,1)S(1)}, bf16[320,256]{1,0:T(8,128)(2,1)S(1)}, u32[]{:S(2)}, u32[]{:S(2)}) collective-permute-start(bf16[320,256]{1,0:T(8,128)(2,1)S(1)} %get-tuple-element.15.own_ref), channel_id=1, source_target_pairs={{0,496},{16,32},{32,16},{48,64},{64,48},{80,96},{96,80},{112,128},... | collective-permute-start | bytes 491528 | tf_op jit(solution)/shard_map/ppermute | solution.py:467
  37.1 6.4 %collective-permute-start.2 = (bf16[320,256]{1,0:T(8,128)(2,1)S(1)}, bf16[320,256]{1,0:T(8,128)(2,1)S(1)}, u32[]{:S(2)}, u32[]{:S(2)}) collective-permute-start(bf16[320,256]{1,0:T(8,128)(2,1)S(1)} %get-tuple-element.15.own_ref), channel_id=1, source_target_pairs={{0,16},{16,0},{32,48},{48,32},{64,80},{80,64},{96,112},{112,96},{1... | collective-permute-start | bytes 491528 | tf_op jit(solution)/shard_map/ppermute | solution.py:467
  43.5 0.0 copy-start.3
  43.5 8.8 %ready.1 = (f32[16,128,128]{2,1,0:T(8,128)}, bf16[3,1024,192]{2,1,0:T(8,128)(2,1)}, bf16[128,256]{1,0:T(8,128)(2,1)}, bf16[256,256]{1,0:T(8,128)(2,1)}) custom-call(s32[1]{0:T(128)} %bitcast.parity_ref, s32[16,16]{1,0:T(8,128)} %src_ref.1, s32[16,16]{1,0:T(8,128)} %kind_ref.1, s32[16]{0:T(128)} %count_ref.1, bf16[16,128,128]{2,1,0:T(8,128)(2,1)} %density_ref.1, ...), custom_call_target="tpu_custom_call" | custom-call | flops 8000000000 | bytes 6291456 | tf_op jit(solution)/shard_map/ready/pallas_call | solution.py:373
  52.3 0.0 copy-start
  52.3 0.0 copy-start.2
  52.3 0.0 copy-start.4
  52.3 4.0 %collective-permute-start = (bf16[128,256]{1,0:T(8,128)(2,1)S(1)}, bf16[128,256]{1,0:T(8,128)(2,1)S(1)}, u32[]{:S(2)}, u32[]{:S(2)}) collective-permute-start(bf16[128,256]{1,0:T(8,128)(2,1)S(1)} %get-tuple-element.19), channel_id=1, source_target_pairs={{0,32},{16,496},{32,64},{48,16},{64,96},{80,48},{96,128},{112,80},... | collective-permute-start | bytes 196616 | tf_op jit(solution)/shard_map/ppermute | solution.py:467
  56.3 1.9 %collective-permute-start.3 = (bf16[128,256]{1,0:T(8,128)(2,1)S(1)}, bf16[128,256]{1,0:T(8,128)(2,1)S(1)}, u32[]{:S(2)}, u32[]{:S(2)}) collective-permute-start(bf16[128,256]{1,0:T(8,128)(2,1)S(1)} %get-tuple-element.19), channel_id=1, source_target_pairs={{0,480},{16,48},{32,0},{48,80},{64,32},{80,112},{96,64},{112,144},... | collective-permute-start | bytes 196616 | tf_op jit(solution)/shard_map/ppermute | solution.py:467
  58.2 0.0 copy-done.3
  58.3 0.0 copy-start.5
  58.3 1.4 %copy-done.5 = bf16[3,1024,192]{2,1,0:T(8,128)(2,1)S(1)} copy-done((bf16[3,1024,192]{2,1,0:T(8,128)(2,1)S(1)}, bf16[3,1024,192]{2,1,0:T(8,128)(2,1)}, u32[]{:S(2)}) %copy-start.5) | copy-done | bytes 1179672
  59.7 0.0 copy-start.8
  59.7 0.0 copy-start.9
  59.7 1.0 %coarse.1 = (f32[1024,256]{1,0:T(8,128)S(1)}, bf16[512,640]{1,0:T(8,128)(2,1)S(1)}, bf16[1024,512]{1,0:T(8,128)(2,1)S(1)}) custom-call(s32[1]{0:T(128)} %bitcast.parity_ref, s32[8,8]{1,0:T(8,128)S(1)} %copy-done.3, bf16[16,136,128]{2,1,0:T(8,128)(2,1)S(1)} %all-to-all-done.gathered_ref, bf16[320,256]{1,0:T(8,128)(2,1)S(1)} %get-tuple-element.15.own_ref, ...), custom_call_target="tpu_custom_call" | custom-call | flops 1000000000 | bytes 4194304 | tf_op jit(solution)/shard_map/coarse/pallas_call | solution.py:431
  60.7 0.0 collective-permute-done.near2_ref
  60.7 2.7 %collective-permute-done.3.far2_ref = bf16[128,256]{1,0:T(8,128)(2,1)S(1)} collective-permute-done((bf16[128,256]{1,0:T(8,128)(2,1)S(1)}, bf16[128,256]{1,0:T(8,128)(2,1)S(1)}, u32[]{:S(2)}, u32[]{:S(2)}) %collective-permute-start.3) | collective-permute-done | bytes 65568 | tf_op jit(solution)/shard_map/ppermute | solution.py:467
  63.4 0.0 collective-permute-done.1.near1_ref
  63.4 0.0 collective-permute-done.2.mate_ref
  63.4 0.0 copy-done
  63.4 0.0 copy-done.2
  63.5 0.0 copy-done.4
  63.5 0.0 copy-done.8
  63.5 0.0 copy-done.9
  63.5 0.0 copy-start.6
  63.5 1.4 %copy-done.6 = bf16[3,1024,192]{2,1,0:T(8,128)(2,1)S(1)} copy-done((bf16[3,1024,192]{2,1,0:T(8,128)(2,1)S(1)}, bf16[3,1024,192]{2,1,0:T(8,128)(2,1)}, u32[]{:S(2)}) %copy-start.6) | copy-done | bytes 1179672
  64.9 0.0 copy-start.7
  64.9 1.2 %copy-done.7 = f32[16,128,128]{2,1,0:T(8,128)S(1)} copy-done((f32[16,128,128]{2,1,0:T(8,128)S(1)}, f32[16,128,128]{2,1,0:T(8,128)}, u32[]{:S(2)}) %copy-start.7) | copy-done | bytes 1048600
  66.1 4.5 %final.1 = bf16[16,128,128]{2,1,0:T(8,128)(2,1)} custom-call(s32[8,8]{1,0:T(8,128)S(1)} %copy-done.4, bf16[3,1024,192]{2,1,0:T(8,128)(2,1)S(1)} %copy-done.6, f32[1024,256]{1,0:T(8,128)S(1)} %get-tuple-element.16.leaf_ref, bf16[512,640]{1,0:T(8,128)(2,1)S(1)} %get-tuple-element.17.hits_ref, bf16[1024,512]{1,0:T(8,128)(2,1)S(1)} %get-tuple-element.18.masks_ref, ...), custom_call_target="tpu_custom_call" | custom-call | flops 4000000000 | bytes 8388608 | tf_op jit(solution)/shard_map/final/pallas_call | solution.py:450
Async XLA Ops:
  2.0 26.3 %all-to-all-start = ((bf16[16,136,128]{2,1,0:T(8,128)(2,1)}), bf16[16,136,128]{2,1,0:T(8,128)(2,1)S(1)}, u32[]{:S(2)}, u32[]{:S(2)}) async-start(bf16[16,136,128]{2,1,0:T(8,128)(2,1)} %payload.1), calls=%async_computation | async-start | bytes 1114112 | tf_op jit(solution)/shard_map/all_to_all | solution.py:498
  28.3 1.2 %copy-start.1 = (bf16[8,256,256]{2,1,0:T(8,128)(2,1)S(1)}, bf16[8,256,256]{2,1,0:T(8,128)(2,1)}, u32[]{:S(2)}) copy-start(bf16[8,256,256]{2,1,0:T(8,128)(2,1)} %shift_ref.3) | copy-start | bytes 3145732
  30.5 32.9 %collective-permute-start.1 = (bf16[320,256]{1,0:T(8,128)(2,1)S(1)}, bf16[320,256]{1,0:T(8,128)(2,1)S(1)}, u32[]{:S(2)}, u32[]{:S(2)}) collective-permute-start(bf16[320,256]{1,0:T(8,128)(2,1)S(1)} %get-tuple-element.15.own_ref), channel_id=1, source_target_pairs={{0,496},{16,32},{32,16},{48,64},{64,48},{80,96},{96,80},{112,128},... | collective-permute-start | bytes 491528 | tf_op jit(solution)/shard_map/ppermute | solution.py:467
  37.1 26.3 %collective-permute-start.2 = (bf16[320,256]{1,0:T(8,128)(2,1)S(1)}, bf16[320,256]{1,0:T(8,128)(2,1)S(1)}, u32[]{:S(2)}, u32[]{:S(2)}) collective-permute-start(bf16[320,256]{1,0:T(8,128)(2,1)S(1)} %get-tuple-element.15.own_ref), channel_id=1, source_target_pairs={{0,16},{16,0},{32,48},{48,32},{64,80},{80,64},{96,112},{112,96},{1... | collective-permute-start | bytes 491528 | tf_op jit(solution)/shard_map/ppermute | solution.py:467
  43.5 14.7 %copy-start.3 = (s32[8,8]{1,0:T(8,128)S(1)}, s32[8,8]{1,0:T(8,128)}, u32[]{:S(2)}) copy-start(s32[8,8]{1,0:T(8,128)} %parent_ref.1) | copy-start | bytes 772
  52.3 11.1 %copy-start = (bf16[16,256,256]{2,1,0:T(8,128)(2,1)S(1)}, bf16[16,256,256]{2,1,0:T(8,128)(2,1)}, u32[]{:S(2)}) copy-start(bf16[16,256,256]{2,1,0:T(8,128)(2,1)} %operators_ref.1) | copy-start | bytes 6291460
  52.3 11.1 %copy-start.2 = (bf16[8,256,256]{2,1,0:T(8,128)(2,1)S(1)}, bf16[8,256,256]{2,1,0:T(8,128)(2,1)}, u32[]{:S(2)}) copy-start(bf16[8,256,256]{2,1,0:T(8,128)(2,1)} %shift_ref.3) | copy-start | bytes 3145732
  52.3 11.1 %copy-start.4 = (s32[8,8]{1,0:T(8,128)S(1)}, s32[8,8]{1,0:T(8,128)}, u32[]{:S(2)}) copy-start(s32[8,8]{1,0:T(8,128)} %octant_ref.1) | copy-start | bytes 772
  52.3 8.4 %collective-permute-start = (bf16[128,256]{1,0:T(8,128)(2,1)S(1)}, bf16[128,256]{1,0:T(8,128)(2,1)S(1)}, u32[]{:S(2)}, u32[]{:S(2)}) collective-permute-start(bf16[128,256]{1,0:T(8,128)(2,1)S(1)} %get-tuple-element.19), channel_id=1, source_target_pairs={{0,32},{16,496},{32,64},{48,16},{64,96},{80,48},{96,128},{112,80},... | collective-permute-start | bytes 196616 | tf_op jit(solution)/shard_map/ppermute | solution.py:467
  56.3 7.1 %collective-permute-start.3 = (bf16[128,256]{1,0:T(8,128)(2,1)S(1)}, bf16[128,256]{1,0:T(8,128)(2,1)S(1)}, u32[]{:S(2)}, u32[]{:S(2)}) collective-permute-start(bf16[128,256]{1,0:T(8,128)(2,1)S(1)} %get-tuple-element.19), channel_id=1, source_target_pairs={{0,480},{16,48},{32,0},{48,80},{64,32},{80,112},{96,64},{112,144},... | collective-permute-start | bytes 196616 | tf_op jit(solution)/shard_map/ppermute | solution.py:467
  58.3 1.4 %copy-start.5 = (bf16[3,1024,192]{2,1,0:T(8,128)(2,1)S(1)}, bf16[3,1024,192]{2,1,0:T(8,128)(2,1)}, u32[]{:S(2)}) copy-start(bf16[3,1024,192]{2,1,0:T(8,128)(2,1)} %get-tuple-element.14.counts_ref) | copy-start | bytes 3538948
  59.7 3.8 %copy-start.8 = (bf16[256,256]{1,0:T(8,128)(2,1)S(1)}, bf16[256,256]{1,0:T(8,128)(2,1)}, u32[]{:S(2)}) copy-start(bf16[256,256]{1,0:T(8,128)(2,1)} %get-tuple-element.21.right_ref) | copy-start | bytes 393220
  59.7 3.8 %copy-start.9 = (bf16[128,256]{1,0:T(8,128)(2,1)S(1)}, bf16[128,256]{1,0:T(8,128)(2,1)}, u32[]{:S(2)}) copy-start(bf16[128,256]{1,0:T(8,128)(2,1)} %get-tuple-element.20.left_ref) | copy-start | bytes 196612
  63.5 1.4 %copy-start.6 = (bf16[3,1024,192]{2,1,0:T(8,128)(2,1)S(1)}, bf16[3,1024,192]{2,1,0:T(8,128)(2,1)}, u32[]{:S(2)}) copy-start(bf16[3,1024,192]{2,1,0:T(8,128)(2,1)} %get-tuple-element.14.counts_ref) | copy-start | bytes 3538948
  64.9 1.2 %copy-start.7 = (f32[16,128,128]{2,1,0:T(8,128)S(1)}, f32[16,128,128]{2,1,0:T(8,128)}, u32[]{:S(2)}) copy-start(f32[16,128,128]{2,1,0:T(8,128)} %get-tuple-element.22.near_ref) | copy-start | bytes 3145732

commit v2 on v1

--- a/solution.py
+++ b/solution.py
@@ -289,10 +289,29 @@
         )
 
 
+def operated(sums, operators_ref):
+    high, low = halves(sums)
+    total = jnp.zeros((2 * LEAVES, COEFFS), F32)
+    for op in range(OPS):
+        rows = slice(op * LEAVES, (op + 1) * LEAVES)
+        total = total + dot(
+            jnp.concatenate([high[rows], low[rows]], axis=0), operators_ref[op]
+        )
+    return total[:LEAVES] + total[LEAVES:]
+
+
+def leaf_kernel(counts_ref, leaf_ref, near1_ref, mate_ref, operators_ref, local_ref):
+    leaf_sums = (
+        leaf_ref[...]
+        + dot(counts_ref[0], near1_ref[PARENTS:, :])
+        + dot(counts_ref[2], mate_ref[PARENTS:, :])
+    )
+    local_ref[...] = operated(leaf_sums, operators_ref)
+
+
 def final_kernel(
     octant_ref,
-    counts_ref,
-    leaf_ref,
+    local_ref,
     hits_ref,
     masks_ref,
     own_ref,
@@ -308,11 +327,6 @@
     out_ref,
     staged,
 ):
-    leaf_sums = (
-        leaf_ref[...]
-        + dot(counts_ref[0], near1_ref[PARENTS:, :])
-        + dot(counts_ref[2], mate_ref[PARENTS:, :])
-    )
     sources = jnp.concatenate(
         [
             near2_ref[...],
@@ -324,18 +338,8 @@
         axis=0,
     )
     coarse_sums = dot(masks_ref[...], dot(hits_ref[...], sources).astype(BF16))
-    leaf_high, leaf_low = halves(leaf_sums)
-    coarse_high, coarse_low = halves(coarse_sums)
-    total = jnp.zeros((4 * LEAVES, COEFFS), F32)
-    for op in range(OPS):
-        rows = slice(op * LEAVES, (op + 1) * LEAVES)
-        stacked = jnp.concatenate(
-            [leaf_high[rows], leaf_low[rows], coarse_high[rows], coarse_low[rows]], axis=0
-        )
-        total = total + dot(stacked, operators_ref[op])
-    local = total[:LEAVES] + total[LEAVES : 2 * LEAVES]
-    coarse_local = total[2 * LEAVES : 3 * LEAVES] + total[3 * LEAVES :]
-    coarse_local = coarse_local.astype(BF16).astype(F32)
+    local = local_ref[...]
+    coarse_local = operated(coarse_sums, operators_ref).astype(BF16).astype(F32)
     octant_of = column_of(octant_ref)
     for octant in range(OCTANTS):
         chosen = jnp.where(octant_of == octant, coarse_local, 0.0).astype(BF16)
@@ -441,6 +445,20 @@
         compiler_params=pltpu.CompilerParams(vmem_limit_bytes=16 * MIB),
         cost_estimate=pl.CostEstimate(
             flops=1000000000, bytes_accessed=4 * MIB, transcendentals=0
+        ),
+    )(*operands)
+
+
+def leaf_call(*operands):
+    return pl.pallas_call(
+        leaf_kernel,
+        name="leaf",
+        out_shape=jax.ShapeDtypeStruct((LEAVES, COEFFS), F32),
+        in_specs=[VMEM] * len(operands),
+        out_specs=VMEM,
+        compiler_params=pltpu.CompilerParams(vmem_limit_bytes=16 * MIB),
+        cost_estimate=pl.CostEstimate(
+            flops=10**9, bytes_accessed=4 * MIB, transcendentals=0
         ),
     )(*operands)
 
@@ -518,10 +536,10 @@
     leaf, hits, masks = coarse_call(
         parity, leaf_parent, gathered, window, counts
     )
+    local = leaf_call(counts, leaf, near1, mate, operators)
     return final_call(
         leaf_octant,
-        counts,
-        leaf,
+        local,
         hits,
         masks,
         window,

time: 71.1 us -> 67.4 us (0.948)
  local copies, waits for them, and re-layouts: 5.28 us -> 3.01 us
  waiting for transfers between devices: 18.8 us -> 17.3 us
    unnamed x20, local copies, waits for them, and re-layouts: 5.28 us -> 3.01 us
    ppermute x4, waiting for transfers between devices: 2.74 us -> 1.24 us  [routed(): return lax.ppermute(value, axis, route)]
    pallas_call x0 -> x1, Pallas kernels: none -> 1.09 us  [leaf_call(): pl.pallas_call(leaf_kernel, name='leaf', out_shape=jax.ShapeDtypeStruct((...]
    pallas_call x1, Pallas kernels: 4.45 us -> 3.58 us  [final_call(): pl.pallas_call(final_kernel, name='final', out_shape=jax.ShapeDtypeStruct...]
  transfers between devices with their start and end apart: 5 -> 5, of which waited for: 2 -> 2; matrix products, arithmetic and copies ran while one was open for 0% -> 0% of each run, Pallas kernels for 14% -> 16%
where the time goes in v2:
time: 67.4 us; the launch traced here: 66.9 us
  starting transfers between devices  29 us (43%)
  Pallas kernels  17.4 us (26%)
  waiting for transfers between devices  17.3 us (26%)
  local copies, waits for them, and re-layouts  3.01 us (4%)
    ppermute x4, starting transfers between devices, routed(): return lax.ppermute(value, axis, route)  18.7 us
    all_to_all x1, waiting for transfers between devices, body(): lax.all_to_all(sent, 'yz', split_axis=0, concat_axis=0, tiled=True)  16.1 us
    all_to_all x1, starting transfers between devices, body(): lax.all_to_all(sent, 'yz', split_axis=0, concat_axis=0, tiled=True)  10.2 us
    pallas_call x1, Pallas kernels, ready_call(): pl.pallas_call(ready_kernel, name='ready', out_shape=(jax.ShapeDtypeStruc...  8.79 us
    pallas_call x1, Pallas kernels, final_call(): pl.pallas_call(final_kernel, name='final', out_shape=jax.ShapeDtypeStruct...  3.58 us
    unnamed x20, local copies, waits for them, and re-layouts  3.01 us
    pallas_call x1, Pallas kernels, payload_call(): pl.pallas_call(payload_kernel, name='payload', out_shape=jax.ShapeDtypeSt...  1.95 us
  transfers between devices with their start and end apart: 5, of which 2 were waited for; matrix products, arithmetic and copies ran while one was open for 0% of the time, Pallas kernels for 16%

profile of v2, /device:TPU:1, one launch (start us, length us, event | category | flops | bytes accessed | tf_op | source)
XLA Modules:
  0.0 66.9 jit_solution(14531652679667729172)
XLA Ops:
  0.0 2.0 %payload.1 = bf16[16,136,128]{2,1,0:T(8,128)(2,1)} custom-call(bf16[64,256]{1,0:T(8,128)(2,1)} %bitcast.8, s32[8,8]{1,0:T(8,128)} %parent_ref.1, s32[8,8]{1,0:T(8,128)} %octant_ref.1, s32[8,8]{1,0:T(8,128)} %bitcast.12, s32[8,8]{1,0:T(8,128)} %bitcast.13), custom_call_target="tpu_custom_call" | custom-call | flops 1000000000 | bytes 1048576 | tf_op jit(solution)/shard_map/payload/pallas_call | solution.py:397
  2.0 10.2 %all-to-all-start = ((bf16[16,136,128]{2,1,0:T(8,128)(2,1)}), bf16[16,136,128]{2,1,0:T(8,128)(2,1)S(1)}, u32[]{:S(2)}, u32[]{:S(2)}) async-start(bf16[16,136,128]{2,1,0:T(8,128)(2,1)} %payload.1), calls=%async_computation | async-start | bytes 1114112 | tf_op jit(solution)/shard_map/all_to_all | solution.py:516
  12.2 16.1 %all-to-all-done.gathered_ref = bf16[16,136,128]{2,1,0:T(8,128)(2,1)S(1)} async-done(((bf16[16,136,128]{2,1,0:T(8,128)(2,1)}), bf16[16,136,128]{2,1,0:T(8,128)(2,1)S(1)}, u32[]{:S(2)}, u32[]{:S(2)}) %all-to-all-start) | async-done | bytes 557088 | tf_op jit(solution)/shard_map/all_to_all | solution.py:516
  28.3 0.0 copy-start.3
  28.3 1.2 %copy-done.3 = bf16[8,256,256]{2,1,0:T(8,128)(2,1)S(1)} copy-done((bf16[8,256,256]{2,1,0:T(8,128)(2,1)S(1)}, bf16[8,256,256]{2,1,0:T(8,128)(2,1)}, u32[]{:S(2)}) %copy-start.3) | copy-done | bytes 1048600
  29.5 1.0 %parents.1 = (bf16[320,256]{1,0:T(8,128)(2,1)S(1)}, bf16[128,256]{1,0:T(8,128)(2,1)S(1)}) custom-call(s32[1]{0:T(128)} %bitcast.7.own_ref, bf16[16,136,128]{2,1,0:T(8,128)(2,1)S(1)} %all-to-all-done.gathered_ref, bf16[8,256,256]{2,1,0:T(8,128)(2,1)S(1)} %copy-done.3), custom_call_target="tpu_custom_call" | custom-call | flops 2000000000 | bytes 2097152 | tf_op jit(solution)/shard_map/parents/pallas_call | solution.py:417
  30.5 6.6 %collective-permute-start = (bf16[320,256]{1,0:T(8,128)(2,1)S(1)}, bf16[320,256]{1,0:T(8,128)(2,1)S(1)}, u32[]{:S(2)}, u32[]{:S(2)}) collective-permute-start(bf16[320,256]{1,0:T(8,128)(2,1)S(1)} %get-tuple-element.15.own_ref), channel_id=1, source_target_pairs={{0,496},{16,32},{32,16},{48,64},{64,48},{80,96},{96,80},{112,128},... | collective-permute-start | bytes 491528 | tf_op jit(solution)/shard_map/ppermute | solution.py:485
  37.1 6.4 %collective-permute-start.1 = (bf16[320,256]{1,0:T(8,128)(2,1)S(1)}, bf16[320,256]{1,0:T(8,128)(2,1)S(1)}, u32[]{:S(2)}, u32[]{:S(2)}) collective-permute-start(bf16[320,256]{1,0:T(8,128)(2,1)S(1)} %get-tuple-element.15.own_ref), channel_id=1, source_target_pairs={{0,16},{16,0},{32,48},{48,32},{64,80},{80,64},{96,112},{112,96},{1... | collective-permute-start | bytes 491528 | tf_op jit(solution)/shard_map/ppermute | solution.py:485
  43.5 0.0 copy-start.5
  43.5 8.8 %ready.1 = (f32[16,128,128]{2,1,0:T(8,128)}, bf16[3,1024,192]{2,1,0:T(8,128)(2,1)}, bf16[128,256]{1,0:T(8,128)(2,1)}, bf16[256,256]{1,0:T(8,128)(2,1)}) custom-call(s32[1]{0:T(128)} %bitcast.parity_ref, s32[16,16]{1,0:T(8,128)} %src_ref.1, s32[16,16]{1,0:T(8,128)} %kind_ref.1, s32[16]{0:T(128)} %count_ref.1, bf16[16,128,128]{2,1,0:T(8,128)(2,1)} %density_ref.1, ...), custom_call_target="tpu_custom_call" | custom-call | flops 8000000000 | bytes 6291456 | tf_op jit(solution)/shard_map/ready/pallas_call | solution.py:377
  52.3 0.0 copy-start
  52.3 3.8 %collective-permute-start.2 = (bf16[128,256]{1,0:T(8,128)(2,1)S(1)}, bf16[128,256]{1,0:T(8,128)(2,1)S(1)}, u32[]{:S(2)}, u32[]{:S(2)}) collective-permute-start(bf16[128,256]{1,0:T(8,128)(2,1)S(1)} %get-tuple-element.19), channel_id=1, source_target_pairs={{0,32},{16,496},{32,64},{48,16},{64,96},{80,48},{96,128},{112,80},... | collective-permute-start | bytes 196616 | tf_op jit(solution)/shard_map/ppermute | solution.py:485
  56.2 1.9 %collective-permute-start.3 = (bf16[128,256]{1,0:T(8,128)(2,1)S(1)}, bf16[128,256]{1,0:T(8,128)(2,1)S(1)}, u32[]{:S(2)}, u32[]{:S(2)}) collective-permute-start(bf16[128,256]{1,0:T(8,128)(2,1)S(1)} %get-tuple-element.19), channel_id=1, source_target_pairs={{0,480},{16,48},{32,0},{48,80},{64,32},{80,112},{96,64},{112,144},... | collective-permute-start | bytes 196616 | tf_op jit(solution)/shard_map/ppermute | solution.py:485
  58.1 0.0 copy-done.5
  58.1 0.0 copy-start.1
  58.1 1.4 %copy-done.1 = bf16[3,1024,192]{2,1,0:T(8,128)(2,1)S(1)} copy-done((bf16[3,1024,192]{2,1,0:T(8,128)(2,1)S(1)}, bf16[3,1024,192]{2,1,0:T(8,128)(2,1)}, u32[]{:S(2)}) %copy-start.1) | copy-done | bytes 1179672
  59.5 0.0 copy-start.2
  59.5 1.0 %coarse.1 = (f32[1024,256]{1,0:T(8,128)S(1)}, bf16[512,640]{1,0:T(8,128)(2,1)S(1)}, bf16[1024,512]{1,0:T(8,128)(2,1)S(1)}) custom-call(s32[1]{0:T(128)} %bitcast.parity_ref, s32[8,8]{1,0:T(8,128)S(1)} %copy-done.5, bf16[16,136,128]{2,1,0:T(8,128)(2,1)S(1)} %all-to-all-done.gathered_ref, bf16[320,256]{1,0:T(8,128)(2,1)S(1)} %get-tuple-element.15.own_ref, ...), custom_call_target="tpu_custom_call" | custom-call | flops 1000000000 | bytes 4194304 | tf_op jit(solution)/shard_map/coarse/pallas_call | solution.py:435
  60.5 0.0 collective-permute-done.near1_ref
  60.5 0.0 collective-permute-done.1.mate_ref
  60.5 0.0 copy-done
  60.6 0.4 copy-done.2
  60.9 0.0 copy-start.4
  60.9 0.0 copy-start.6
  60.9 0.0 copy-start.7
  60.9 0.0 copy-start.8
  60.9 0.0 copy-start.9
  60.9 1.1 %leaf.1.local_ref = f32[64,256]{1,0:T(8,128)S(1)} custom-call(bf16[3,1024,192]{2,1,0:T(8,128)(2,1)S(1)} %copy-done.2, f32[1024,256]{1,0:T(8,128)S(1)} %get-tuple-element.16.leaf_ref, bf16[320,256]{1,0:T(8,128)(2,1)S(1)} %collective-permute-done.near1_ref, bf16[320,256]{1,0:T(8,128)(2,1)S(1)} %collective-permute-done.1.mate_ref, bf16[16,256,256]{2,1,0:T(8,128)(2,1)S(1)} %copy-done), custom_call_target="tpu_custom_call" | custom-call | flops 1000000000 | bytes 4194304 | tf_op jit(solution)/shard_map/leaf/pallas_call | solution.py:453
  62.0 0.0 collective-permute-done.2.near2_ref
  62.0 1.2 %collective-permute-done.3.far2_ref = bf16[128,256]{1,0:T(8,128)(2,1)S(1)} collective-permute-done((bf16[128,256]{1,0:T(8,128)(2,1)S(1)}, bf16[128,256]{1,0:T(8,128)(2,1)S(1)}, u32[]{:S(2)}, u32[]{:S(2)}) %collective-permute-start.3) | collective-permute-done | bytes 65568 | tf_op jit(solution)/shard_map/ppermute | solution.py:485
  63.3 0.0 copy-done.4
  63.3 0.0 copy-done.6
  63.3 0.0 copy-done.7
  63.3 0.0 copy-done.8
  63.3 0.0 copy-done.9
  63.3 3.6 %final.1 = bf16[16,128,128]{2,1,0:T(8,128)(2,1)} custom-call(s32[8,8]{1,0:T(8,128)S(1)} %copy-done.6, f32[64,256]{1,0:T(8,128)S(1)} %leaf.1.local_ref, bf16[512,640]{1,0:T(8,128)(2,1)S(1)} %get-tuple-element.17.hits_ref, bf16[1024,512]{1,0:T(8,128)(2,1)S(1)} %get-tuple-element.18.masks_ref, bf16[320,256]{1,0:T(8,128)(2,1)S(1)} %get-tuple-element.15.own_ref, ...), custom_call_target="tpu_custom_call" | custom-call | flops 4000000000 | bytes 8388608 | tf_op jit(solution)/shard_map/final/pallas_call | solution.py:468
Async XLA Ops:
  2.0 26.3 %all-to-all-start = ((bf16[16,136,128]{2,1,0:T(8,128)(2,1)}), bf16[16,136,128]{2,1,0:T(8,128)(2,1)S(1)}, u32[]{:S(2)}, u32[]{:S(2)}) async-start(bf16[16,136,128]{2,1,0:T(8,128)(2,1)} %payload.1), calls=%async_computation | async-start | bytes 1114112 | tf_op jit(solution)/shard_map/all_to_all | solution.py:516
  28.3 1.2 %copy-start.3 = (bf16[8,256,256]{2,1,0:T(8,128)(2,1)S(1)}, bf16[8,256,256]{2,1,0:T(8,128)(2,1)}, u32[]{:S(2)}) copy-start(bf16[8,256,256]{2,1,0:T(8,128)(2,1)} %shift_ref.3) | copy-start | bytes 3145732
  30.5 30.0 %collective-permute-start = (bf16[320,256]{1,0:T(8,128)(2,1)S(1)}, bf16[320,256]{1,0:T(8,128)(2,1)S(1)}, u32[]{:S(2)}, u32[]{:S(2)}) collective-permute-start(bf16[320,256]{1,0:T(8,128)(2,1)S(1)} %get-tuple-element.15.own_ref), channel_id=1, source_target_pairs={{0,496},{16,32},{32,16},{48,64},{64,48},{80,96},{96,80},{112,128},... | collective-permute-start | bytes 491528 | tf_op jit(solution)/shard_map/ppermute | solution.py:485
  37.1 23.4 %collective-permute-start.1 = (bf16[320,256]{1,0:T(8,128)(2,1)S(1)}, bf16[320,256]{1,0:T(8,128)(2,1)S(1)}, u32[]{:S(2)}, u32[]{:S(2)}) collective-permute-start(bf16[320,256]{1,0:T(8,128)(2,1)S(1)} %get-tuple-element.15.own_ref), channel_id=1, source_target_pairs={{0,16},{16,0},{32,48},{48,32},{64,80},{80,64},{96,112},{112,96},{1... | collective-permute-start | bytes 491528 | tf_op jit(solution)/shard_map/ppermute | solution.py:485
  43.5 14.6 %copy-start.5 = (s32[8,8]{1,0:T(8,128)S(1)}, s32[8,8]{1,0:T(8,128)}, u32[]{:S(2)}) copy-start(s32[8,8]{1,0:T(8,128)} %parent_ref.1) | copy-start | bytes 772
  52.3 8.2 %copy-start = (bf16[16,256,256]{2,1,0:T(8,128)(2,1)S(1)}, bf16[16,256,256]{2,1,0:T(8,128)(2,1)}, u32[]{:S(2)}) copy-start(bf16[16,256,256]{2,1,0:T(8,128)(2,1)} %operators_ref.3) | copy-start | bytes 6291460
  52.3 9.7 %collective-permute-start.2 = (bf16[128,256]{1,0:T(8,128)(2,1)S(1)}, bf16[128,256]{1,0:T(8,128)(2,1)S(1)}, u32[]{:S(2)}, u32[]{:S(2)}) collective-permute-start(bf16[128,256]{1,0:T(8,128)(2,1)S(1)} %get-tuple-element.19), channel_id=1, source_target_pairs={{0,32},{16,496},{32,64},{48,16},{64,96},{80,48},{96,128},{112,80},... | collective-permute-start | bytes 196616 | tf_op jit(solution)/shard_map/ppermute | solution.py:485
  56.2 7.1 %collective-permute-start.3 = (bf16[128,256]{1,0:T(8,128)(2,1)S(1)}, bf16[128,256]{1,0:T(8,128)(2,1)S(1)}, u32[]{:S(2)}, u32[]{:S(2)}) collective-permute-start(bf16[128,256]{1,0:T(8,128)(2,1)S(1)} %get-tuple-element.19), channel_id=1, source_target_pairs={{0,480},{16,48},{32,0},{48,80},{64,32},{80,112},{96,64},{112,144},... | collective-permute-start | bytes 196616 | tf_op jit(solution)/shard_map/ppermute | solution.py:485
  58.1 1.4 %copy-start.1 = (bf16[3,1024,192]{2,1,0:T(8,128)(2,1)S(1)}, bf16[3,1024,192]{2,1,0:T(8,128)(2,1)}, u32[]{:S(2)}) copy-start(bf16[3,1024,192]{2,1,0:T(8,128)(2,1)} %get-tuple-element.14.counts_ref) | copy-start | bytes 3538948
  59.5 1.4 %copy-start.2 = (bf16[3,1024,192]{2,1,0:T(8,128)(2,1)S(1)}, bf16[3,1024,192]{2,1,0:T(8,128)(2,1)}, u32[]{:S(2)}) copy-start(bf16[3,1024,192]{2,1,0:T(8,128)(2,1)} %get-tuple-element.14.counts_ref) | copy-start | bytes 3538948
  60.9 2.4 %copy-start.4 = (bf16[8,256,256]{2,1,0:T(8,128)(2,1)S(1)}, bf16[8,256,256]{2,1,0:T(8,128)(2,1)}, u32[]{:S(2)}) copy-start(bf16[8,256,256]{2,1,0:T(8,128)(2,1)} %shift_ref.3) | copy-start | bytes 3145732
  60.9 2.4 %copy-start.6 = (s32[8,8]{1,0:T(8,128)S(1)}, s32[8,8]{1,0:T(8,128)}, u32[]{:S(2)}) copy-start(s32[8,8]{1,0:T(8,128)} %octant_ref.1) | copy-start | bytes 772
  60.9 2.4 %copy-start.7 = (f32[16,128,128]{2,1,0:T(8,128)S(1)}, f32[16,128,128]{2,1,0:T(8,128)}, u32[]{:S(2)}) copy-start(f32[16,128,128]{2,1,0:T(8,128)} %get-tuple-element.22.near_ref) | copy-start | bytes 3145732
  60.9 2.4 %copy-start.8 = (bf16[256,256]{1,0:T(8,128)(2,1)S(1)}, bf16[256,256]{1,0:T(8,128)(2,1)}, u32[]{:S(2)}) copy-start(bf16[256,256]{1,0:T(8,128)(2,1)} %get-tuple-element.21.right_ref) | copy-start | bytes 393220
  60.9 2.4 %copy-start.9 = (bf16[128,256]{1,0:T(8,128)(2,1)S(1)}, bf16[128,256]{1,0:T(8,128)(2,1)}, u32[]{:S(2)}) copy-start(bf16[128,256]{1,0:T(8,128)(2,1)} %get-tuple-element.20.left_ref) | copy-start | bytes 196612
